TPU v7x, 32 devices: a whole 2x2x4 slice. The times are simulated.
32 devices in a mesh: elem: 8 (over z, y), chan: 4 (over x, core).
Axes of the slice: x: 2, y: 2, z: 4, core: 2. Of those that a mesh axis runs over, the one named last changes fastest.
Arguments:
- voltages: bfloat16 [2, 1024, 19584], P(None, ('elem', 'chan')), may hold values from -6 to 6
- delays: int32 [1024], P(('elem', 'chan')), may hold values from 0 to 127
- prototype: bfloat16 [16, 1024], replicated, may hold values from -1.5 to 1.5
- subband_map: int32 [16], replicated, may hold values from 0 to 1023, as said below
- beam_weights: bfloat16 [512, 2, 16, 1024], P('elem', None, 'chan'), may hold values from -0.25 to 0.25
Outputs:
- element_power: bfloat16 [1024, 1024], P(('elem', 'chan'))
- beam_voltages: float32 [2, 64, 512], P(None, 'chan', 'elem')
Inputs may be any that keep to these rules, and one draw needn't show every extreme that they name: `subband_map`: distinct channel numbers.
All inputs are finite; a program needn't handle non-finite values.
Results may differ from a plain program's by a relative error of at most 0.007.
Values may be sent and summed in bfloat16 or wider, within the bound.
A program may use at most 128 MiB of HBM per device.

v0:
```python
import math
import jax
import jax.numpy as jnp
from jax import lax
from jax.sharding import PartitionSpec as P

FRAMES = 4
SUB_C = 4


def filtered(voltages, delays, prototype):
    tap_count, chan_count = prototype.shape
    blocks = FRAMES + tap_count - 1
    window_len = blocks * chan_count

    def window(samples, offset):
        return lax.dynamic_slice_in_dim(samples, offset, window_len, 0)

    segments = jax.vmap(jax.vmap(window, in_axes=(0, 0)), in_axes=(0, None))(voltages, delays)
    segments = segments.reshape(voltages.shape[0], voltages.shape[1], blocks, chan_count)
    coeffs = prototype.astype(jnp.float32)
    running = jnp.zeros((voltages.shape[0], voltages.shape[1], FRAMES, chan_count), jnp.float32)
    for tap_index in range(tap_count):
        running = running + coeffs[tap_index] * segments[
            :, :, tap_index : tap_index + FRAMES, :
        ].astype(jnp.float32)
    return running.astype(jnp.bfloat16)


def spectra(filtered_wave):
    part_count, elem_count, frame_count, chan_count = filtered_wave.shape
    counter = jnp.arange(chan_count, dtype=jnp.int32)
    residue = counter[:, None] * counter[None, :] % chan_count
    radians = residue.astype(jnp.float32) * (2.0 * math.pi / chan_count)
    factor = 1.0 / math.sqrt(chan_count)
    basis = jnp.concatenate([jnp.cos(radians) * factor, jnp.sin(radians) * factor], axis=1)
    basis_high = basis.astype(jnp.bfloat16)
    basis_low = (basis - basis_high.astype(jnp.float32)).astype(jnp.bfloat16)
    flattened = filtered_wave.reshape(part_count * elem_count * frame_count, chan_count)
    product = jnp.dot(flattened, basis_high, preferred_element_type=jnp.float32)
    product = product + jnp.dot(flattened, basis_low, preferred_element_type=jnp.float32)
    product = product.reshape(part_count, elem_count, frame_count, 2, chan_count)
    spec_real = product[0, :, :, 0] + product[1, :, :, 1]
    spec_imag = product[1, :, :, 0] - product[0, :, :, 1]
    return (spec_real, spec_imag)


def beam_terms(spectra_part, weight_part):
    weight_real = weight_part[:, 0]
    weight_imag = weight_part[:, 1]

    def contract(spectral, weighting):
        return jnp.einsum("sfe,bse->sfb", spectral, weighting, preferred_element_type=jnp.float32)

    out_real = contract(spectra_part[0], weight_real) - contract(spectra_part[1], weight_imag)
    out_imag = contract(spectra_part[1], weight_real) + contract(spectra_part[0], weight_imag)
    return jnp.stack([out_real, out_imag])


def on_device(voltages, delays, prototype, subband_map, beam_weights):
    filtered_wave = filtered(voltages, delays, prototype)
    spec_real, spec_imag = spectra(filtered_wave)
    element_power = jnp.mean(spec_real * spec_real + spec_imag * spec_imag, axis=1).astype(
        jnp.bfloat16
    )
    picked = jnp.stack([spec_real[:, :, subband_map], spec_imag[:, :, subband_map]]).astype(
        jnp.bfloat16
    )
    picked = jnp.transpose(picked, (0, 3, 2, 1))
    turned = lax.all_to_all(picked, "chan", split_axis=1, concat_axis=3, tiled=True)
    local_beams = beam_weights.shape[0]
    summed = beam_terms(lax.all_gather(turned, "elem", axis=3, tiled=True), beam_weights)
    beam_voltages = summed.reshape(2, SUB_C * FRAMES, local_beams)
    return (element_power, beam_voltages)


def solution(mesh):
    return jax.shard_map(
        on_device,
        mesh=mesh,
        in_specs=(
            P(None, ("elem", "chan"), None),
            P(("elem", "chan")),
            P(),
            P(),
            P("elem", None, "chan", None),
        ),
        out_specs=(P(("elem", "chan"), None), P(None, "chan", "elem")),
        check_vma=False,
    )
```

profile of v0, /device:TPU:0, one launch (start us, length us, event | category | flops | bytes accessed | tf_op | source)
XLA Modules:
  0.0 187.4 jit_solution(4113093099833259249)
XLA Ops:
  0.7 17.8 %sine_multiply_fusion = (f32[1024,1024]{1,0:T(8,128)}, f32[1024,1024]{1,0:T(8,128)}) fusion(), kind=kLoop, calls=%fused_computation.14 | loop fusion | flops 16777216 | bytes 8388608 | tf_op jit(solution)/shard_map/mul | solution.py:36
  18.5 1.9 %copy.22 = bf16[2,32,19584]{2,0,1:T(2,128)(2,1)S(1)} copy(bf16[2,32,19584]{2,1,0:T(8,128)(2,1)S(1)} %copy-done.2) | data formatting | bytes 5013504
  20.5 85.7 %while.1 = (s32[]{:T(128)}, bf16[2,32,19584]{2,0,1:T(2,128)(2,1)S(1)}, s32[32,2]{0,1:T(2,128)S(1)}, bf16[32,2,19456]{2,1,0:T(2,128)(2,1)}, s32[]{:T(128)}) while((s32[]{:T(128)}, bf16[2,32,19584]{2,0,1:T(2,128)(2,1)S(1)}, s32[32,2]{0,1:T(2,128)S(1)}, bf16[32,2,19456]{2,1,0:T(2,128)(2,1)}, s32[]{:T(128)}) %tuple.49), condition=%wide.while_cond, body=%wide.while_body.sunk | while | flops 2 | bytes 157281 | solution.py:17
  20.6 0.5 fusion.23
  21.2 2.1 %bitcast_dynamic-update-slice_fusion.2 = bf16[32,2,19456]{2,1,0:T(2,128)(2,1)} fusion(bf16[32,2,19456]{2,1,0:T(2,128)(2,1)} %get-tuple-element.97, s32[]{:T(128)} %get-tuple-element.94, bf16[2,32,19584]{2,0,1:T(2,128)(2,1)S(1)} %get-tuple-element.100, s32[]{:T(128)} %bitcast.72, s32[]{:T(128)} %bitcast.73), kind=kLoop, calls=%fused_computation.2.clone.1 | loop fusion | bytes 157184 | tf_op jit(solution)/shard_map/vmap(vmap())/gather
  23.3 0.5 fusion.23
  23.8 2.1 %bitcast_dynamic-update-slice_fusion.2 = bf16[32,2,19456]{2,1,0:T(2,128)(2,1)} fusion(bf16[32,2,19456]{2,1,0:T(2,128)(2,1)} %get-tuple-element.97, s32[]{:T(128)} %get-tuple-element.94, bf16[2,32,19584]{2,0,1:T(2,128)(2,1)S(1)} %get-tuple-element.100, s32[]{:T(128)} %bitcast.72, s32[]{:T(128)} %bitcast.73), kind=kLoop, calls=%fused_computation.2.clone.1 | loop fusion | bytes 157184 | tf_op jit(solution)/shard_map/vmap(vmap())/gather
  26.0 0.5 fusion.23
  26.5 2.1 %bitcast_dynamic-update-slice_fusion.2 = bf16[32,2,19456]{2,1,0:T(2,128)(2,1)} fusion(bf16[32,2,19456]{2,1,0:T(2,128)(2,1)} %get-tuple-element.97, s32[]{:T(128)} %get-tuple-element.94, bf16[2,32,19584]{2,0,1:T(2,128)(2,1)S(1)} %get-tuple-element.100, s32[]{:T(128)} %bitcast.72, s32[]{:T(128)} %bitcast.73), kind=kLoop, calls=%fused_computation.2.clone.1 | loop fusion | bytes 157184 | tf_op jit(solution)/shard_map/vmap(vmap())/gather
  28.7 0.5 fusion.23
  29.2 2.1 %bitcast_dynamic-update-slice_fusion.2 = bf16[32,2,19456]{2,1,0:T(2,128)(2,1)} fusion(bf16[32,2,19456]{2,1,0:T(2,128)(2,1)} %get-tuple-element.97, s32[]{:T(128)} %get-tuple-element.94, bf16[2,32,19584]{2,0,1:T(2,128)(2,1)S(1)} %get-tuple-element.100, s32[]{:T(128)} %bitcast.72, s32[]{:T(128)} %bitcast.73), kind=kLoop, calls=%fused_computation.2.clone.1 | loop fusion | bytes 157184 | tf_op jit(solution)/shard_map/vmap(vmap())/gather
  31.9 2.1 %bitcast_dynamic-update-slice_fusion.2 = bf16[32,2,19456]{2,1,0:T(2,128)(2,1)} fusion(bf16[32,2,19456]{2,1,0:T(2,128)(2,1)} %get-tuple-element.97, s32[]{:T(128)} %get-tuple-element.94, bf16[2,32,19584]{2,0,1:T(2,128)(2,1)S(1)} %get-tuple-element.100, s32[]{:T(128)} %bitcast.72, s32[]{:T(128)} %bitcast.73), kind=kLoop, calls=%fused_computation.2.clone.1 | loop fusion | bytes 157184 | tf_op jit(solution)/shard_map/vmap(vmap())/gather
  34.0 0.5 fusion.23
  34.5 2.1 %bitcast_dynamic-update-slice_fusion.2 = bf16[32,2,19456]{2,1,0:T(2,128)(2,1)} fusion(bf16[32,2,19456]{2,1,0:T(2,128)(2,1)} %get-tuple-element.97, s32[]{:T(128)} %get-tuple-element.94, bf16[2,32,19584]{2,0,1:T(2,128)(2,1)S(1)} %get-tuple-element.100, s32[]{:T(128)} %bitcast.72, s32[]{:T(128)} %bitcast.73), kind=kLoop, calls=%fused_computation.2.clone.1 | loop fusion | bytes 157184 | tf_op jit(solution)/shard_map/vmap(vmap())/gather
  36.7 0.5 fusion.23
  37.2 2.1 %bitcast_dynamic-update-slice_fusion.2 = bf16[32,2,19456]{2,1,0:T(2,128)(2,1)} fusion(bf16[32,2,19456]{2,1,0:T(2,128)(2,1)} %get-tuple-element.97, s32[]{:T(128)} %get-tuple-element.94, bf16[2,32,19584]{2,0,1:T(2,128)(2,1)S(1)} %get-tuple-element.100, s32[]{:T(128)} %bitcast.72, s32[]{:T(128)} %bitcast.73), kind=kLoop, calls=%fused_computation.2.clone.1 | loop fusion | bytes 157184 | tf_op jit(solution)/shard_map/vmap(vmap())/gather
  39.9 2.1 %bitcast_dynamic-update-slice_fusion.2 = bf16[32,2,19456]{2,1,0:T(2,128)(2,1)} fusion(bf16[32,2,19456]{2,1,0:T(2,128)(2,1)} %get-tuple-element.97, s32[]{:T(128)} %get-tuple-element.94, bf16[2,32,19584]{2,0,1:T(2,128)(2,1)S(1)} %get-tuple-element.100, s32[]{:T(128)} %bitcast.72, s32[]{:T(128)} %bitcast.73), kind=kLoop, calls=%fused_computation.2.clone.1 | loop fusion | bytes 157184 | tf_op jit(solution)/shard_map/vmap(vmap())/gather
  42.6 2.1 %bitcast_dynamic-update-slice_fusion.2 = bf16[32,2,19456]{2,1,0:T(2,128)(2,1)} fusion(bf16[32,2,19456]{2,1,0:T(2,128)(2,1)} %get-tuple-element.97, s32[]{:T(128)} %get-tuple-element.94, bf16[2,32,19584]{2,0,1:T(2,128)(2,1)S(1)} %get-tuple-element.100, s32[]{:T(128)} %bitcast.72, s32[]{:T(128)} %bitcast.73), kind=kLoop, calls=%fused_computation.2.clone.1 | loop fusion | bytes 157184 | tf_op jit(solution)/shard_map/vmap(vmap())/gather
  45.3 2.1 %bitcast_dynamic-update-slice_fusion.2 = bf16[32,2,19456]{2,1,0:T(2,128)(2,1)} fusion(bf16[32,2,19456]{2,1,0:T(2,128)(2,1)} %get-tuple-element.97, s32[]{:T(128)} %get-tuple-element.94, bf16[2,32,19584]{2,0,1:T(2,128)(2,1)S(1)} %get-tuple-element.100, s32[]{:T(128)} %bitcast.72, s32[]{:T(128)} %bitcast.73), kind=kLoop, calls=%fused_computation.2.clone.1 | loop fusion | bytes 157184 | tf_op jit(solution)/shard_map/vmap(vmap())/gather
  48.0 2.1 %bitcast_dynamic-update-slice_fusion.2 = bf16[32,2,19456]{2,1,0:T(2,128)(2,1)} fusion(bf16[32,2,19456]{2,1,0:T(2,128)(2,1)} %get-tuple-element.97, s32[]{:T(128)} %get-tuple-element.94, bf16[2,32,19584]{2,0,1:T(2,128)(2,1)S(1)} %get-tuple-element.100, s32[]{:T(128)} %bitcast.72, s32[]{:T(128)} %bitcast.73), kind=kLoop, calls=%fused_computation.2.clone.1 | loop fusion | bytes 157184 | tf_op jit(solution)/shard_map/vmap(vmap())/gather
  50.6 2.1 %bitcast_dynamic-update-slice_fusion.2 = bf16[32,2,19456]{2,1,0:T(2,128)(2,1)} fusion(bf16[32,2,19456]{2,1,0:T(2,128)(2,1)} %get-tuple-element.97, s32[]{:T(128)} %get-tuple-element.94, bf16[2,32,19584]{2,0,1:T(2,128)(2,1)S(1)} %get-tuple-element.100, s32[]{:T(128)} %bitcast.72, s32[]{:T(128)} %bitcast.73), kind=kLoop, calls=%fused_computation.2.clone.1 | loop fusion | bytes 157184 | tf_op jit(solution)/shard_map/vmap(vmap())/gather
  53.3 2.1 %bitcast_dynamic-update-slice_fusion.2 = bf16[32,2,19456]{2,1,0:T(2,128)(2,1)} fusion(bf16[32,2,19456]{2,1,0:T(2,128)(2,1)} %get-tuple-element.97, s32[]{:T(128)} %get-tuple-element.94, bf16[2,32,19584]{2,0,1:T(2,128)(2,1)S(1)} %get-tuple-element.100, s32[]{:T(128)} %bitcast.72, s32[]{:T(128)} %bitcast.73), kind=kLoop, calls=%fused_computation.2.clone.1 | loop fusion | bytes 157184 | tf_op jit(solution)/shard_map/vmap(vmap())/gather
  56.0 2.1 %bitcast_dynamic-update-slice_fusion.2 = bf16[32,2,19456]{2,1,0:T(2,128)(2,1)} fusion(bf16[32,2,19456]{2,1,0:T(2,128)(2,1)} %get-tuple-element.97, s32[]{:T(128)} %get-tuple-element.94, bf16[2,32,19584]{2,0,1:T(2,128)(2,1)S(1)} %get-tuple-element.100, s32[]{:T(128)} %bitcast.72, s32[]{:T(128)} %bitcast.73), kind=kLoop, calls=%fused_computation.2.clone.1 | loop fusion | bytes 157184 | tf_op jit(solution)/shard_map/vmap(vmap())/gather
  58.7 2.1 %bitcast_dynamic-update-slice_fusion.2 = bf16[32,2,19456]{2,1,0:T(2,128)(2,1)} fusion(bf16[32,2,19456]{2,1,0:T(2,128)(2,1)} %get-tuple-element.97, s32[]{:T(128)} %get-tuple-element.94, bf16[2,32,19584]{2,0,1:T(2,128)(2,1)S(1)} %get-tuple-element.100, s32[]{:T(128)} %bitcast.72, s32[]{:T(128)} %bitcast.73), kind=kLoop, calls=%fused_computation.2.clone.1 | loop fusion | bytes 157184 | tf_op jit(solution)/shard_map/vmap(vmap())/gather
  61.4 2.1 %bitcast_dynamic-update-slice_fusion.2 = bf16[32,2,19456]{2,1,0:T(2,128)(2,1)} fusion(bf16[32,2,19456]{2,1,0:T(2,128)(2,1)} %get-tuple-element.97, s32[]{:T(128)} %get-tuple-element.94, bf16[2,32,19584]{2,0,1:T(2,128)(2,1)S(1)} %get-tuple-element.100, s32[]{:T(128)} %bitcast.72, s32[]{:T(128)} %bitcast.73), kind=kLoop, calls=%fused_computation.2.clone.1 | loop fusion | bytes 157184 | tf_op jit(solution)/shard_map/vmap(vmap())/gather
  64.0 2.1 %bitcast_dynamic-update-slice_fusion.2 = bf16[32,2,19456]{2,1,0:T(2,128)(2,1)} fusion(bf16[32,2,19456]{2,1,0:T(2,128)(2,1)} %get-tuple-element.97, s32[]{:T(128)} %get-tuple-element.94, bf16[2,32,19584]{2,0,1:T(2,128)(2,1)S(1)} %get-tuple-element.100, s32[]{:T(128)} %bitcast.72, s32[]{:T(128)} %bitcast.73), kind=kLoop, calls=%fused_computation.2.clone.1 | loop fusion | bytes 157184 | tf_op jit(solution)/shard_map/vmap(vmap())/gather
  66.7 2.1 %bitcast_dynamic-update-slice_fusion.2 = bf16[32,2,19456]{2,1,0:T(2,128)(2,1)} fusion(bf16[32,2,19456]{2,1,0:T(2,128)(2,1)} %get-tuple-element.97, s32[]{:T(128)} %get-tuple-element.94, bf16[2,32,19584]{2,0,1:T(2,128)(2,1)S(1)} %get-tuple-element.100, s32[]{:T(128)} %bitcast.72, s32[]{:T(128)} %bitcast.73), kind=kLoop, calls=%fused_computation.2.clone.1 | loop fusion | bytes 157184 | tf_op jit(solution)/shard_map/vmap(vmap())/gather
  69.4 2.1 %bitcast_dynamic-update-slice_fusion.2 = bf16[32,2,19456]{2,1,0:T(2,128)(2,1)} fusion(bf16[32,2,19456]{2,1,0:T(2,128)(2,1)} %get-tuple-element.97, s32[]{:T(128)} %get-tuple-element.94, bf16[2,32,19584]{2,0,1:T(2,128)(2,1)S(1)} %get-tuple-element.100, s32[]{:T(128)} %bitcast.72, s32[]{:T(128)} %bitcast.73), kind=kLoop, calls=%fused_computation.2.clone.1 | loop fusion | bytes 157184 | tf_op jit(solution)/shard_map/vmap(vmap())/gather
  72.1 2.1 %bitcast_dynamic-update-slice_fusion.2 = bf16[32,2,19456]{2,1,0:T(2,128)(2,1)} fusion(bf16[32,2,19456]{2,1,0:T(2,128)(2,1)} %get-tuple-element.97, s32[]{:T(128)} %get-tuple-element.94, bf16[2,32,19584]{2,0,1:T(2,128)(2,1)S(1)} %get-tuple-element.100, s32[]{:T(128)} %bitcast.72, s32[]{:T(128)} %bitcast.73), kind=kLoop, calls=%fused_computation.2.clone.1 | loop fusion | bytes 157184 | tf_op jit(solution)/shard_map/vmap(vmap())/gather
  74.7 2.1 %bitcast_dynamic-update-slice_fusion.2 = bf16[32,2,19456]{2,1,0:T(2,128)(2,1)} fusion(bf16[32,2,19456]{2,1,0:T(2,128)(2,1)} %get-tuple-element.97, s32[]{:T(128)} %get-tuple-element.94, bf16[2,32,19584]{2,0,1:T(2,128)(2,1)S(1)} %get-tuple-element.100, s32[]{:T(128)} %bitcast.72, s32[]{:T(128)} %bitcast.73), kind=kLoop, calls=%fused_computation.2.clone.1 | loop fusion | bytes 157184 | tf_op jit(solution)/shard_map/vmap(vmap())/gather
  77.4 2.1 %bitcast_dynamic-update-slice_fusion.2 = bf16[32,2,19456]{2,1,0:T(2,128)(2,1)} fusion(bf16[32,2,19456]{2,1,0:T(2,128)(2,1)} %get-tuple-element.97, s32[]{:T(128)} %get-tuple-element.94, bf16[2,32,19584]{2,0,1:T(2,128)(2,1)S(1)} %get-tuple-element.100, s32[]{:T(128)} %bitcast.72, s32[]{:T(128)} %bitcast.73), kind=kLoop, calls=%fused_computation.2.clone.1 | loop fusion | bytes 157184 | tf_op jit(solution)/shard_map/vmap(vmap())/gather
  80.1 2.1 %bitcast_dynamic-update-slice_fusion.2 = bf16[32,2,19456]{2,1,0:T(2,128)(2,1)} fusion(bf16[32,2,19456]{2,1,0:T(2,128)(2,1)} %get-tuple-element.97, s32[]{:T(128)} %get-tuple-element.94, bf16[2,32,19584]{2,0,1:T(2,128)(2,1)S(1)} %get-tuple-element.100, s32[]{:T(128)} %bitcast.72, s32[]{:T(128)} %bitcast.73), kind=kLoop, calls=%fused_computation.2.clone.1 | loop fusion | bytes 157184 | tf_op jit(solution)/shard_map/vmap(vmap())/gather
  82.8 2.1 %bitcast_dynamic-update-slice_fusion.2 = bf16[32,2,19456]{2,1,0:T(2,128)(2,1)} fusion(bf16[32,2,19456]{2,1,0:T(2,128)(2,1)} %get-tuple-element.97, s32[]{:T(128)} %get-tuple-element.94, bf16[2,32,19584]{2,0,1:T(2,128)(2,1)S(1)} %get-tuple-element.100, s32[]{:T(128)} %bitcast.72, s32[]{:T(128)} %bitcast.73), kind=kLoop, calls=%fused_computation.2.clone.1 | loop fusion | bytes 157184 | tf_op jit(solution)/shard_map/vmap(vmap())/gather
  85.4 2.1 %bitcast_dynamic-update-slice_fusion.2 = bf16[32,2,19456]{2,1,0:T(2,128)(2,1)} fusion(bf16[32,2,19456]{2,1,0:T(2,128)(2,1)} %get-tuple-element.97, s32[]{:T(128)} %get-tuple-element.94, bf16[2,32,19584]{2,0,1:T(2,128)(2,1)S(1)} %get-tuple-element.100, s32[]{:T(128)} %bitcast.72, s32[]{:T(128)} %bitcast.73), kind=kLoop, calls=%fused_computation.2.clone.1 | loop fusion | bytes 157184 | tf_op jit(solution)/shard_map/vmap(vmap())/gather
  88.1 2.1 %bitcast_dynamic-update-slice_fusion.2 = bf16[32,2,19456]{2,1,0:T(2,128)(2,1)} fusion(bf16[32,2,19456]{2,1,0:T(2,128)(2,1)} %get-tuple-element.97, s32[]{:T(128)} %get-tuple-element.94, bf16[2,32,19584]{2,0,1:T(2,128)(2,1)S(1)} %get-tuple-element.100, s32[]{:T(128)} %bitcast.72, s32[]{:T(128)} %bitcast.73), kind=kLoop, calls=%fused_computation.2.clone.1 | loop fusion | bytes 157184 | tf_op jit(solution)/shard_map/vmap(vmap())/gather
  90.8 2.1 %bitcast_dynamic-update-slice_fusion.2 = bf16[32,2,19456]{2,1,0:T(2,128)(2,1)} fusion(bf16[32,2,19456]{2,1,0:T(2,128)(2,1)} %get-tuple-element.97, s32[]{:T(128)} %get-tuple-element.94, bf16[2,32,19584]{2,0,1:T(2,128)(2,1)S(1)} %get-tuple-element.100, s32[]{:T(128)} %bitcast.72, s32[]{:T(128)} %bitcast.73), kind=kLoop, calls=%fused_computation.2.clone.1 | loop fusion | bytes 157184 | tf_op jit(solution)/shard_map/vmap(vmap())/gather
  93.5 2.1 %bitcast_dynamic-update-slice_fusion.2 = bf16[32,2,19456]{2,1,0:T(2,128)(2,1)} fusion(bf16[32,2,19456]{2,1,0:T(2,128)(2,1)} %get-tuple-element.97, s32[]{:T(128)} %get-tuple-element.94, bf16[2,32,19584]{2,0,1:T(2,128)(2,1)S(1)} %get-tuple-element.100, s32[]{:T(128)} %bitcast.72, s32[]{:T(128)} %bitcast.73), kind=kLoop, calls=%fused_computation.2.clone.1 | loop fusion | bytes 157184 | tf_op jit(solution)/shard_map/vmap(vmap())/gather
  96.1 2.1 %bitcast_dynamic-update-slice_fusion.2 = bf16[32,2,19456]{2,1,0:T(2,128)(2,1)} fusion(bf16[32,2,19456]{2,1,0:T(2,128)(2,1)} %get-tuple-element.97, s32[]{:T(128)} %get-tuple-element.94, bf16[2,32,19584]{2,0,1:T(2,128)(2,1)S(1)} %get-tuple-element.100, s32[]{:T(128)} %bitcast.72, s32[]{:T(128)} %bitcast.73), kind=kLoop, calls=%fused_computation.2.clone.1 | loop fusion | bytes 157184 | tf_op jit(solution)/shard_map/vmap(vmap())/gather
  98.8 2.1 %bitcast_dynamic-update-slice_fusion.2 = bf16[32,2,19456]{2,1,0:T(2,128)(2,1)} fusion(bf16[32,2,19456]{2,1,0:T(2,128)(2,1)} %get-tuple-element.97, s32[]{:T(128)} %get-tuple-element.94, bf16[2,32,19584]{2,0,1:T(2,128)(2,1)S(1)} %get-tuple-element.100, s32[]{:T(128)} %bitcast.72, s32[]{:T(128)} %bitcast.73), kind=kLoop, calls=%fused_computation.2.clone.1 | loop fusion | bytes 157184 | tf_op jit(solution)/shard_map/vmap(vmap())/gather
  101.5 2.1 %bitcast_dynamic-update-slice_fusion.2 = bf16[32,2,19456]{2,1,0:T(2,128)(2,1)} fusion(bf16[32,2,19456]{2,1,0:T(2,128)(2,1)} %get-tuple-element.97, s32[]{:T(128)} %get-tuple-element.94, bf16[2,32,19584]{2,0,1:T(2,128)(2,1)S(1)} %get-tuple-element.100, s32[]{:T(128)} %bitcast.72, s32[]{:T(128)} %bitcast.73), kind=kLoop, calls=%fused_computation.2.clone.1 | loop fusion | bytes 157184 | tf_op jit(solution)/shard_map/vmap(vmap())/gather
  104.2 2.1 %bitcast_dynamic-update-slice_fusion.2 = bf16[32,2,19456]{2,1,0:T(2,128)(2,1)} fusion(bf16[32,2,19456]{2,1,0:T(2,128)(2,1)} %get-tuple-element.97, s32[]{:T(128)} %get-tuple-element.94, bf16[2,32,19584]{2,0,1:T(2,128)(2,1)S(1)} %get-tuple-element.100, s32[]{:T(128)} %bitcast.72, s32[]{:T(128)} %bitcast.73), kind=kLoop, calls=%fused_computation.2.clone.1 | loop fusion | bytes 157184 | tf_op jit(solution)/shard_map/vmap(vmap())/gather
  106.2 3.6 %copy.23 = bf16[2,32,19456]{2,1,0:T(8,128)(2,1)} copy(bf16[2,32,19456]{2,0,1:T(2,128)(2,1)} %bitcast.74) | data formatting | bytes 4980736 | tf_op jit(solution)/shard_map/vmap(vmap())/gather | solution.py:17
  109.9 3.3 %reshape.36 = bf16[2,32,19,1024]{3,2,1,0:T(8,128)(2,1)S(1)} reshape(bf16[2,32,19456]{2,1,0:T(8,128)(2,1)} %copy.23) | data formatting | bytes 4980736 | tf_op jit(solution)/shard_map/reshape | solution.py:20
  113.2 5.1 %add_convert_fusion = bf16[2,32,4,1024]{3,2,1,0:T(4,128)(2,1)} fusion(bf16[2,32,19,1024]{3,2,1,0:T(8,128)(2,1)S(1)} %reshape.36, f32[1024]{0:T(1024)S(1)} %bitcast.94, f32[1024]{0:T(1024)S(1)} %bitcast.93, f32[1024]{0:T(1024)S(1)} %bitcast.92, f32[1024]{0:T(1024)S(1)} %bitcast.91, f32[1024]{0:T(1024)S(1)} %bitcast.90, f32[1024]{0:T(1024)S(1)} %bitcast.89, ...), kind=kLoop, calls=%fused_computation.26 | loop fusion | flops 12582912 | bytes 8978432 | tf_op jit(solution)/shard_map/convert_element_type | solution.py:27
  118.3 1.2 reshape.37
  119.5 4.8 %fusion.1 = f32[256,2048]{1,0:T(8,128)S(1)} fusion(bf16[256,1024]{1,0:T(8,128)(2,1)S(1)} %reshape.37, f32[1024,1024]{1,0:T(8,128)} %get-tuple-element.55, f32[1024,1024]{1,0:T(8,128)} %get-tuple-element.56), kind=kOutput, calls=%fused_computation.10 | convolution fusion | flops 1082130432 | bytes 11010048 | tf_op jit(solution)/shard_map/dot_general | solution.py:40
  124.4 1.0 copy-done.1
  125.4 1.3 fusion.10
  126.7 2.8 %reshape.38 = f32[2,32,4,2,1024]{4,3,2,1,0:T(2,128)} reshape(f32[256,2048]{1,0:T(8,128)S(1)} %fusion.10) | data formatting | bytes 4194304 | tf_op jit(solution)/shard_map/reshape | solution.py:42
  129.5 5.4 %fusion.17 = (f32[1,32,4,1,1024]{4,3,2,1,0:T(1,128)S(1)}, f32[1,32,4,1,1024]{4,3,2,1,0:T(1,128)S(1)}, f32[1,32,4,1,1024]{4,3,2,1,0:T(1,128)}, f32[1,32,4,1,1024]{4,3,2,1,0:T(1,128)}) fusion(f32[2,32,4,2,1024]{4,3,2,1,0:T(2,128)} %reshape.38), kind=kLoop, calls=%fused_computation.46 | loop fusion | bytes 4194304 | tf_op jit(solution)/shard_map/slice | solution.py:44
  134.9 2.7 %copy.34 = f32[1,32,4,1,1024]{1,2,4,3,0:T(4,128)S(1)} copy(f32[1,32,4,1,1024]{4,3,2,1,0:T(1,128)} %get-tuple-element.36) | data formatting | bytes 1048576
  137.6 3.3 %copy.35 = f32[1,32,4,1,1024]{1,2,4,3,0:T(4,128)} copy(f32[1,32,4,1,1024]{4,3,2,1,0:T(1,128)} %get-tuple-element.35) | data formatting | bytes 1048576
  141.0 2.4 %copy.36 = f32[1,32,4,1,1024]{1,2,4,3,0:T(4,128)} copy(f32[1,32,4,1,1024]{4,3,2,1,0:T(1,128)S(1)} %get-tuple-element.34) | data formatting | bytes 1048576
  143.3 2.4 %copy.37 = f32[1,32,4,1,1024]{1,2,4,3,0:T(4,128)} copy(f32[1,32,4,1,1024]{4,3,2,1,0:T(1,128)S(1)} %get-tuple-element.33) | data formatting | bytes 1048576
  145.8 5.7 %add_reduce_fusion = (f32[32,1024]{0,1:T(8,128)S(1)}, bf16[32,4,1024]{0,1,2:T(4,128)(2,1)}, bf16[32,4,1024]{0,1,2:T(4,128)(2,1)}) fusion(f32[1,32,4,1,1024]{1,2,4,3,0:T(4,128)S(1)} %copy.34, f32[1,32,4,1,1024]{1,2,4,3,0:T(4,128)} %copy.35, f32[1,32,4,1,1024]{1,2,4,3,0:T(4,128)} %copy.36, f32[1,32,4,1,1024]{1,2,4,3,0:T(4,128)} %copy.37), kind=kLoop, calls=%fused_computation.21 | loop fusion | flops 1015808 | bytes 2752512 | tf_op jit(solution)/shard_map/reduce_sum | solution.py:63
  151.4 1.8 gather_fusion.1
  153.2 1.8 gather_fusion
  155.1 0.7 reshape.78
  155.8 4.2 %all-to-all-start = ((bf16[4,2,512]{2,1,0:T(2,128)(2,1)}), bf16[4,2,512]{2,1,0:T(2,128)(2,1)S(1)}, u32[]{:S(2)}, u32[]{:S(2)}) async-start(bf16[4,2,512]{2,1,0:T(2,128)(2,1)} %reshape.78), calls=%async_computation | async-start | bytes 16384 | tf_op jit(solution)/shard_map/all_to_all | solution.py:70
  160.0 1.6 fusion.18
  161.6 0.8 copy.33
  162.4 1.5 all-to-all-done
  164.0 21.6 %all_gather.3 = bf16[2,4,4,1024]{3,2,1,0:T(4,128)(2,1)S(1)} all-gather(bf16[2,4,4,128]{3,2,1,0:T(4,128)(2,1)S(1)} %all_to_all.16), channel_id=1, replica_groups=mesh['elem'=8,'chan'=4] {'elem'}, dimensions={3}, use_global_device_ids=true | all-gather | bytes 73728 | tf_op jit(solution)/shard_map/all_gather | solution.py:72
  186.8 0.6 pad_maximum_fusion.1
  (86 shorter events, 17.8 us)
Async XLA Ops:
  0.6 17.8 %copy-start.3 = (bf16[16,1024]{1,0:T(8,128)(2,1)S(1)}, bf16[16,1024]{1,0:T(8,128)(2,1)}, u32[]{:S(2)}) copy-start(bf16[16,1024]{1,0:T(8,128)(2,1)} %param.7) | copy-start | bytes 98308
  0.7 17.9 %copy-start.2 = (bf16[2,32,19584]{2,1,0:T(8,128)(2,1)S(1)}, bf16[2,32,19584]{2,1,0:T(8,128)(2,1)}, u32[]{:S(2)}) copy-start(bf16[2,32,19584]{2,1,0:T(8,128)(2,1)} %param.5) | copy-start | bytes 7520260
  18.5 2.0 %copy-start.4 = (s32[32]{0:T(128)S(1)}, s32[32]{0:T(128)}, u32[]{:S(2)}) copy-start(s32[32]{0:T(128)} %param.6) | copy-start | bytes 388
  119.5 4.9 %copy-start = (f32[1024,1024]{1,0:T(8,128)S(1)}, f32[1024,1024]{1,0:T(8,128)}, u32[]{:S(2)}) copy-start(f32[1024,1024]{1,0:T(8,128)} %get-tuple-element.55) | copy-start | bytes 12582916
  119.5 5.9 %copy-start.1 = (f32[1024,1024]{1,0:T(8,128)S(1)}, f32[1024,1024]{1,0:T(8,128)}, u32[]{:S(2)}) copy-start(f32[1024,1024]{1,0:T(8,128)} %get-tuple-element.56) | copy-start | bytes 12582916
  137.6 8.1 %copy-start.5 = (s32[16]{0:T(128)S(1)}, s32[16]{0:T(128)}, u32[]{:S(2)}) copy-start(s32[16]{0:T(128)} %param.8) | copy-start | bytes 196
  155.8 8.1 %all-to-all-start = ((bf16[4,2,512]{2,1,0:T(2,128)(2,1)}), bf16[4,2,512]{2,1,0:T(2,128)(2,1)S(1)}, u32[]{:S(2)}, u32[]{:S(2)}) async-start(bf16[4,2,512]{2,1,0:T(2,128)(2,1)} %reshape.78), calls=%async_computation | async-start | bytes 16384 | tf_op jit(solution)/shard_map/all_to_all | solution.py:70
where the time goes:
time: 189 us; the launch traced here: 187 us
  local copies, waits for them, and re-layouts  123 us (65%)
  other arithmetic  29.3 us (16%)
  blocking collectives  21.6 us (11%)
  matrix products  7.36 us (4%)
  starting transfers between devices  4.24 us (2%)
    gather x96, local copies, waits for them, and re-layouts  85.6 us
    all_gather x1, blocking collectives, on_device(): lax.all_gather(turned, 'elem', axis=3, tiled=True)  21.6 us
    mul x1, other arithmetic, spectra(): jnp.sin(radians) * factor  17.8 us
    unnamed x21, local copies, waits for them, and re-layouts  15.3 us
    reduce_sum x1, other arithmetic, on_device(): jnp.mean(spec_real * spec_real + spec_imag * spec_imag, axis=1)  5.67 us
    slice x1, local copies, waits for them, and re-layouts, spectra(): spec_imag = product[1, :, :, 0] - product[0, :, :, 1]  5.38 us
    convert_element_type x1, other arithmetic, filtered(): return running.astype(jnp.bfloat16)  5.1 us
    dot_general x1, matrix products, spectra(): product = jnp.dot(flattened, basis_high, preferred_element_type=jnp.float32)  4.85 us
  transfers between devices with their start and end apart: 1, of which 1 were waited for; matrix products, arithmetic and copies ran while one was open for 1% of the time, Pallas kernels for 0%

commit v1 on v0

--- a/solution.py
+++ b/solution.py
@@ -69,7 +69,7 @@
     picked = jnp.transpose(picked, (0, 3, 2, 1))
     turned = lax.all_to_all(picked, "chan", split_axis=1, concat_axis=3, tiled=True)
     local_beams = beam_weights.shape[0]
-    summed = beam_terms(lax.all_gather(turned, "elem", axis=3, tiled=True), beam_weights)
+    summed = beam_terms(jnp.concatenate(lax.all_gather(turned, "elem"), axis=3), beam_weights)
     beam_voltages = summed.reshape(2, SUB_C * FRAMES, local_beams)
     return (element_power, beam_voltages)
 

time: 189 us -> 195 us (1.032)
  blocking collectives: 21.6 us -> 31.3 us
  local copies, waits for them, and re-layouts: 123 us -> 120 us
    all_gather x1, blocking collectives: 21.6 us -> 31.3 us  [on_device(): lax.all_gather(turned, 'elem')]
    gather x96, local copies, waits for them, and re-layouts: 85.6 us -> 82.8 us
where the time goes in v1:
time: 195 us; the launch traced here: 194 us
  local copies, waits for them, and re-layouts  120 us (62%)
  blocking collectives  31.3 us (16%)
  other arithmetic  29.3 us (15%)
  matrix products  7.36 us (4%)
  starting transfers between devices  4.24 us (2%)
    gather x96, local copies, waits for them, and re-layouts  82.8 us
    all_gather x1, blocking collectives, on_device(): lax.all_gather(turned, 'elem')  31.3 us
    mul x1, other arithmetic, spectra(): jnp.sin(radians) * factor  17.8 us
    unnamed x21, local copies, waits for them, and re-layouts  15.3 us
    reduce_sum x1, other arithmetic, on_device(): jnp.mean(spec_real * spec_real + spec_imag * spec_imag, axis=1)  5.68 us
    slice x1, local copies, waits for them, and re-layouts, spectra(): spec_imag = product[1, :, :, 0] - product[0, :, :, 1]  5.37 us
    convert_element_type x1, other arithmetic, filtered(): return running.astype(jnp.bfloat16)  5.1 us
    dot_general x1, matrix products, spectra(): product = jnp.dot(flattened, basis_high, preferred_element_type=jnp.float32)  4.85 us
  transfers between devices with their start and end apart: 1, of which 1 were waited for; matrix products, arithmetic and copies ran while one was open for 1% of the time, Pallas kernels for 0%

profile of v1, /device:TPU:0, one launch (start us, length us, event | category | flops | bytes accessed | tf_op | source)
XLA Modules:
  0.0 194.4 jit_solution(5556805223871747941)
XLA Ops:
  0.7 17.8 %sine_multiply_fusion = (f32[1024,1024]{1,0:T(8,128)}, f32[1024,1024]{1,0:T(8,128)}) fusion(), kind=kLoop, calls=%fused_computation.14 | loop fusion | flops 16777216 | bytes 8388608 | tf_op jit(solution)/shard_map/mul | solution.py:36
  18.5 1.9 copy.24
  20.5 82.9 %while.1 = (s32[]{:T(128)}, bf16[2,32,19584]{2,0,1:T(2,128)(2,1)S(1)}, s32[32,2]{0,1:T(2,128)S(1)}, bf16[32,2,19456]{2,1,0:T(2,128)(2,1)}, s32[]{:T(128)}) while((s32[]{:T(128)}, bf16[2,32,19584]{2,0,1:T(2,128)(2,1)S(1)}, s32[32,2]{0,1:T(2,128)S(1)}, bf16[32,2,19456]{2,1,0:T(2,128)(2,1)}, s32[]{:T(128)}) %tuple.50), condition=%wide.while_cond, body=%wide.while_body.sunk | while | flops 2 | bytes 157281 | solution.py:17
  20.6 0.5 fusion.28
  21.1 2.0 %bitcast_dynamic-update-slice_fusion.2 = bf16[32,2,19456]{2,1,0:T(2,128)(2,1)} fusion(bf16[32,2,19456]{2,1,0:T(2,128)(2,1)} %get-tuple-element.99, s32[]{:T(128)} %get-tuple-element.96, bf16[2,32,19584]{2,0,1:T(2,128)(2,1)S(1)} %get-tuple-element.102, s32[]{:T(128)} %bitcast.73, s32[]{:T(128)} %bitcast.74), kind=kLoop, calls=%fused_computation.2.clone.1 | loop fusion | bytes 157184 | tf_op jit(solution)/shard_map/vmap(vmap())/gather
  23.7 2.0 %bitcast_dynamic-update-slice_fusion.2 = bf16[32,2,19456]{2,1,0:T(2,128)(2,1)} fusion(bf16[32,2,19456]{2,1,0:T(2,128)(2,1)} %get-tuple-element.99, s32[]{:T(128)} %get-tuple-element.96, bf16[2,32,19584]{2,0,1:T(2,128)(2,1)S(1)} %get-tuple-element.102, s32[]{:T(128)} %bitcast.73, s32[]{:T(128)} %bitcast.74), kind=kLoop, calls=%fused_computation.2.clone.1 | loop fusion | bytes 157184 | tf_op jit(solution)/shard_map/vmap(vmap())/gather
  25.8 0.5 fusion.28
  26.3 2.0 %bitcast_dynamic-update-slice_fusion.2 = bf16[32,2,19456]{2,1,0:T(2,128)(2,1)} fusion(bf16[32,2,19456]{2,1,0:T(2,128)(2,1)} %get-tuple-element.99, s32[]{:T(128)} %get-tuple-element.96, bf16[2,32,19584]{2,0,1:T(2,128)(2,1)S(1)} %get-tuple-element.102, s32[]{:T(128)} %bitcast.73, s32[]{:T(128)} %bitcast.74), kind=kLoop, calls=%fused_computation.2.clone.1 | loop fusion | bytes 157184 | tf_op jit(solution)/shard_map/vmap(vmap())/gather
  28.9 2.0 %bitcast_dynamic-update-slice_fusion.2 = bf16[32,2,19456]{2,1,0:T(2,128)(2,1)} fusion(bf16[32,2,19456]{2,1,0:T(2,128)(2,1)} %get-tuple-element.99, s32[]{:T(128)} %get-tuple-element.96, bf16[2,32,19584]{2,0,1:T(2,128)(2,1)S(1)} %get-tuple-element.102, s32[]{:T(128)} %bitcast.73, s32[]{:T(128)} %bitcast.74), kind=kLoop, calls=%fused_computation.2.clone.1 | loop fusion | bytes 157184 | tf_op jit(solution)/shard_map/vmap(vmap())/gather
  31.5 2.0 %bitcast_dynamic-update-slice_fusion.2 = bf16[32,2,19456]{2,1,0:T(2,128)(2,1)} fusion(bf16[32,2,19456]{2,1,0:T(2,128)(2,1)} %get-tuple-element.99, s32[]{:T(128)} %get-tuple-element.96, bf16[2,32,19584]{2,0,1:T(2,128)(2,1)S(1)} %get-tuple-element.102, s32[]{:T(128)} %bitcast.73, s32[]{:T(128)} %bitcast.74), kind=kLoop, calls=%fused_computation.2.clone.1 | loop fusion | bytes 157184 | tf_op jit(solution)/shard_map/vmap(vmap())/gather
  34.1 2.0 %bitcast_dynamic-update-slice_fusion.2 = bf16[32,2,19456]{2,1,0:T(2,128)(2,1)} fusion(bf16[32,2,19456]{2,1,0:T(2,128)(2,1)} %get-tuple-element.99, s32[]{:T(128)} %get-tuple-element.96, bf16[2,32,19584]{2,0,1:T(2,128)(2,1)S(1)} %get-tuple-element.102, s32[]{:T(128)} %bitcast.73, s32[]{:T(128)} %bitcast.74), kind=kLoop, calls=%fused_computation.2.clone.1 | loop fusion | bytes 157184 | tf_op jit(solution)/shard_map/vmap(vmap())/gather
  36.7 2.0 %bitcast_dynamic-update-slice_fusion.2 = bf16[32,2,19456]{2,1,0:T(2,128)(2,1)} fusion(bf16[32,2,19456]{2,1,0:T(2,128)(2,1)} %get-tuple-element.99, s32[]{:T(128)} %get-tuple-element.96, bf16[2,32,19584]{2,0,1:T(2,128)(2,1)S(1)} %get-tuple-element.102, s32[]{:T(128)} %bitcast.73, s32[]{:T(128)} %bitcast.74), kind=kLoop, calls=%fused_computation.2.clone.1 | loop fusion | bytes 157184 | tf_op jit(solution)/shard_map/vmap(vmap())/gather
  38.8 0.5 fusion.28
  39.3 2.0 %bitcast_dynamic-update-slice_fusion.2 = bf16[32,2,19456]{2,1,0:T(2,128)(2,1)} fusion(bf16[32,2,19456]{2,1,0:T(2,128)(2,1)} %get-tuple-element.99, s32[]{:T(128)} %get-tuple-element.96, bf16[2,32,19584]{2,0,1:T(2,128)(2,1)S(1)} %get-tuple-element.102, s32[]{:T(128)} %bitcast.73, s32[]{:T(128)} %bitcast.74), kind=kLoop, calls=%fused_computation.2.clone.1 | loop fusion | bytes 157184 | tf_op jit(solution)/shard_map/vmap(vmap())/gather
  41.9 2.0 %bitcast_dynamic-update-slice_fusion.2 = bf16[32,2,19456]{2,1,0:T(2,128)(2,1)} fusion(bf16[32,2,19456]{2,1,0:T(2,128)(2,1)} %get-tuple-element.99, s32[]{:T(128)} %get-tuple-element.96, bf16[2,32,19584]{2,0,1:T(2,128)(2,1)S(1)} %get-tuple-element.102, s32[]{:T(128)} %bitcast.73, s32[]{:T(128)} %bitcast.74), kind=kLoop, calls=%fused_computation.2.clone.1 | loop fusion | bytes 157184 | tf_op jit(solution)/shard_map/vmap(vmap())/gather
  44.5 2.0 %bitcast_dynamic-update-slice_fusion.2 = bf16[32,2,19456]{2,1,0:T(2,128)(2,1)} fusion(bf16[32,2,19456]{2,1,0:T(2,128)(2,1)} %get-tuple-element.99, s32[]{:T(128)} %get-tuple-element.96, bf16[2,32,19584]{2,0,1:T(2,128)(2,1)S(1)} %get-tuple-element.102, s32[]{:T(128)} %bitcast.73, s32[]{:T(128)} %bitcast.74), kind=kLoop, calls=%fused_computation.2.clone.1 | loop fusion | bytes 157184 | tf_op jit(solution)/shard_map/vmap(vmap())/gather
  47.1 2.0 %bitcast_dynamic-update-slice_fusion.2 = bf16[32,2,19456]{2,1,0:T(2,128)(2,1)} fusion(bf16[32,2,19456]{2,1,0:T(2,128)(2,1)} %get-tuple-element.99, s32[]{:T(128)} %get-tuple-element.96, bf16[2,32,19584]{2,0,1:T(2,128)(2,1)S(1)} %get-tuple-element.102, s32[]{:T(128)} %bitcast.73, s32[]{:T(128)} %bitcast.74), kind=kLoop, calls=%fused_computation.2.clone.1 | loop fusion | bytes 157184 | tf_op jit(solution)/shard_map/vmap(vmap())/gather
  49.1 0.5 fusion.28
  49.6 2.0 %bitcast_dynamic-update-slice_fusion.2 = bf16[32,2,19456]{2,1,0:T(2,128)(2,1)} fusion(bf16[32,2,19456]{2,1,0:T(2,128)(2,1)} %get-tuple-element.99, s32[]{:T(128)} %get-tuple-element.96, bf16[2,32,19584]{2,0,1:T(2,128)(2,1)S(1)} %get-tuple-element.102, s32[]{:T(128)} %bitcast.73, s32[]{:T(128)} %bitcast.74), kind=kLoop, calls=%fused_computation.2.clone.1 | loop fusion | bytes 157184 | tf_op jit(solution)/shard_map/vmap(vmap())/gather
  52.2 2.0 %bitcast_dynamic-update-slice_fusion.2 = bf16[32,2,19456]{2,1,0:T(2,128)(2,1)} fusion(bf16[32,2,19456]{2,1,0:T(2,128)(2,1)} %get-tuple-element.99, s32[]{:T(128)} %get-tuple-element.96, bf16[2,32,19584]{2,0,1:T(2,128)(2,1)S(1)} %get-tuple-element.102, s32[]{:T(128)} %bitcast.73, s32[]{:T(128)} %bitcast.74), kind=kLoop, calls=%fused_computation.2.clone.1 | loop fusion | bytes 157184 | tf_op jit(solution)/shard_map/vmap(vmap())/gather
  54.8 2.0 %bitcast_dynamic-update-slice_fusion.2 = bf16[32,2,19456]{2,1,0:T(2,128)(2,1)} fusion(bf16[32,2,19456]{2,1,0:T(2,128)(2,1)} %get-tuple-element.99, s32[]{:T(128)} %get-tuple-element.96, bf16[2,32,19584]{2,0,1:T(2,128)(2,1)S(1)} %get-tuple-element.102, s32[]{:T(128)} %bitcast.73, s32[]{:T(128)} %bitcast.74), kind=kLoop, calls=%fused_computation.2.clone.1 | loop fusion | bytes 157184 | tf_op jit(solution)/shard_map/vmap(vmap())/gather
  57.4 2.0 %bitcast_dynamic-update-slice_fusion.2 = bf16[32,2,19456]{2,1,0:T(2,128)(2,1)} fusion(bf16[32,2,19456]{2,1,0:T(2,128)(2,1)} %get-tuple-element.99, s32[]{:T(128)} %get-tuple-element.96, bf16[2,32,19584]{2,0,1:T(2,128)(2,1)S(1)} %get-tuple-element.102, s32[]{:T(128)} %bitcast.73, s32[]{:T(128)} %bitcast.74), kind=kLoop, calls=%fused_computation.2.clone.1 | loop fusion | bytes 157184 | tf_op jit(solution)/shard_map/vmap(vmap())/gather
  60.0 2.0 %bitcast_dynamic-update-slice_fusion.2 = bf16[32,2,19456]{2,1,0:T(2,128)(2,1)} fusion(bf16[32,2,19456]{2,1,0:T(2,128)(2,1)} %get-tuple-element.99, s32[]{:T(128)} %get-tuple-element.96, bf16[2,32,19584]{2,0,1:T(2,128)(2,1)S(1)} %get-tuple-element.102, s32[]{:T(128)} %bitcast.73, s32[]{:T(128)} %bitcast.74), kind=kLoop, calls=%fused_computation.2.clone.1 | loop fusion | bytes 157184 | tf_op jit(solution)/shard_map/vmap(vmap())/gather
  62.1 0.5 fusion.28
  62.6 2.0 %bitcast_dynamic-update-slice_fusion.2 = bf16[32,2,19456]{2,1,0:T(2,128)(2,1)} fusion(bf16[32,2,19456]{2,1,0:T(2,128)(2,1)} %get-tuple-element.99, s32[]{:T(128)} %get-tuple-element.96, bf16[2,32,19584]{2,0,1:T(2,128)(2,1)S(1)} %get-tuple-element.102, s32[]{:T(128)} %bitcast.73, s32[]{:T(128)} %bitcast.74), kind=kLoop, calls=%fused_computation.2.clone.1 | loop fusion | bytes 157184 | tf_op jit(solution)/shard_map/vmap(vmap())/gather
  65.2 2.0 %bitcast_dynamic-update-slice_fusion.2 = bf16[32,2,19456]{2,1,0:T(2,128)(2,1)} fusion(bf16[32,2,19456]{2,1,0:T(2,128)(2,1)} %get-tuple-element.99, s32[]{:T(128)} %get-tuple-element.96, bf16[2,32,19584]{2,0,1:T(2,128)(2,1)S(1)} %get-tuple-element.102, s32[]{:T(128)} %bitcast.73, s32[]{:T(128)} %bitcast.74), kind=kLoop, calls=%fused_computation.2.clone.1 | loop fusion | bytes 157184 | tf_op jit(solution)/shard_map/vmap(vmap())/gather
  67.8 2.0 %bitcast_dynamic-update-slice_fusion.2 = bf16[32,2,19456]{2,1,0:T(2,128)(2,1)} fusion(bf16[32,2,19456]{2,1,0:T(2,128)(2,1)} %get-tuple-element.99, s32[]{:T(128)} %get-tuple-element.96, bf16[2,32,19584]{2,0,1:T(2,128)(2,1)S(1)} %get-tuple-element.102, s32[]{:T(128)} %bitcast.73, s32[]{:T(128)} %bitcast.74), kind=kLoop, calls=%fused_computation.2.clone.1 | loop fusion | bytes 157184 | tf_op jit(solution)/shard_map/vmap(vmap())/gather
  69.8 0.5 fusion.28
  70.3 2.0 %bitcast_dynamic-update-slice_fusion.2 = bf16[32,2,19456]{2,1,0:T(2,128)(2,1)} fusion(bf16[32,2,19456]{2,1,0:T(2,128)(2,1)} %get-tuple-element.99, s32[]{:T(128)} %get-tuple-element.96, bf16[2,32,19584]{2,0,1:T(2,128)(2,1)S(1)} %get-tuple-element.102, s32[]{:T(128)} %bitcast.73, s32[]{:T(128)} %bitcast.74), kind=kLoop, calls=%fused_computation.2.clone.1 | loop fusion | bytes 157184 | tf_op jit(solution)/shard_map/vmap(vmap())/gather
  72.9 2.0 %bitcast_dynamic-update-slice_fusion.2 = bf16[32,2,19456]{2,1,0:T(2,128)(2,1)} fusion(bf16[32,2,19456]{2,1,0:T(2,128)(2,1)} %get-tuple-element.99, s32[]{:T(128)} %get-tuple-element.96, bf16[2,32,19584]{2,0,1:T(2,128)(2,1)S(1)} %get-tuple-element.102, s32[]{:T(128)} %bitcast.73, s32[]{:T(128)} %bitcast.74), kind=kLoop, calls=%fused_computation.2.clone.1 | loop fusion | bytes 157184 | tf_op jit(solution)/shard_map/vmap(vmap())/gather
  75.5 2.0 %bitcast_dynamic-update-slice_fusion.2 = bf16[32,2,19456]{2,1,0:T(2,128)(2,1)} fusion(bf16[32,2,19456]{2,1,0:T(2,128)(2,1)} %get-tuple-element.99, s32[]{:T(128)} %get-tuple-element.96, bf16[2,32,19584]{2,0,1:T(2,128)(2,1)S(1)} %get-tuple-element.102, s32[]{:T(128)} %bitcast.73, s32[]{:T(128)} %bitcast.74), kind=kLoop, calls=%fused_computation.2.clone.1 | loop fusion | bytes 157184 | tf_op jit(solution)/shard_map/vmap(vmap())/gather
  78.1 2.0 %bitcast_dynamic-update-slice_fusion.2 = bf16[32,2,19456]{2,1,0:T(2,128)(2,1)} fusion(bf16[32,2,19456]{2,1,0:T(2,128)(2,1)} %get-tuple-element.99, s32[]{:T(128)} %get-tuple-element.96, bf16[2,32,19584]{2,0,1:T(2,128)(2,1)S(1)} %get-tuple-element.102, s32[]{:T(128)} %bitcast.73, s32[]{:T(128)} %bitcast.74), kind=kLoop, calls=%fused_computation.2.clone.1 | loop fusion | bytes 157184 | tf_op jit(solution)/shard_map/vmap(vmap())/gather
  80.7 2.0 %bitcast_dynamic-update-slice_fusion.2 = bf16[32,2,19456]{2,1,0:T(2,128)(2,1)} fusion(bf16[32,2,19456]{2,1,0:T(2,128)(2,1)} %get-tuple-element.99, s32[]{:T(128)} %get-tuple-element.96, bf16[2,32,19584]{2,0,1:T(2,128)(2,1)S(1)} %get-tuple-element.102, s32[]{:T(128)} %bitcast.73, s32[]{:T(128)} %bitcast.74), kind=kLoop, calls=%fused_computation.2.clone.1 | loop fusion | bytes 157184 | tf_op jit(solution)/shard_map/vmap(vmap())/gather
  83.3 2.0 %bitcast_dynamic-update-slice_fusion.2 = bf16[32,2,19456]{2,1,0:T(2,128)(2,1)} fusion(bf16[32,2,19456]{2,1,0:T(2,128)(2,1)} %get-tuple-element.99, s32[]{:T(128)} %get-tuple-element.96, bf16[2,32,19584]{2,0,1:T(2,128)(2,1)S(1)} %get-tuple-element.102, s32[]{:T(128)} %bitcast.73, s32[]{:T(128)} %bitcast.74), kind=kLoop, calls=%fused_computation.2.clone.1 | loop fusion | bytes 157184 | tf_op jit(solution)/shard_map/vmap(vmap())/gather
  85.9 2.0 %bitcast_dynamic-update-slice_fusion.2 = bf16[32,2,19456]{2,1,0:T(2,128)(2,1)} fusion(bf16[32,2,19456]{2,1,0:T(2,128)(2,1)} %get-tuple-element.99, s32[]{:T(128)} %get-tuple-element.96, bf16[2,32,19584]{2,0,1:T(2,128)(2,1)S(1)} %get-tuple-element.102, s32[]{:T(128)} %bitcast.73, s32[]{:T(128)} %bitcast.74), kind=kLoop, calls=%fused_computation.2.clone.1 | loop fusion | bytes 157184 | tf_op jit(solution)/shard_map/vmap(vmap())/gather
  88.5 2.0 %bitcast_dynamic-update-slice_fusion.2 = bf16[32,2,19456]{2,1,0:T(2,128)(2,1)} fusion(bf16[32,2,19456]{2,1,0:T(2,128)(2,1)} %get-tuple-element.99, s32[]{:T(128)} %get-tuple-element.96, bf16[2,32,19584]{2,0,1:T(2,128)(2,1)S(1)} %get-tuple-element.102, s32[]{:T(128)} %bitcast.73, s32[]{:T(128)} %bitcast.74), kind=kLoop, calls=%fused_computation.2.clone.1 | loop fusion | bytes 157184 | tf_op jit(solution)/shard_map/vmap(vmap())/gather
  91.1 2.0 %bitcast_dynamic-update-slice_fusion.2 = bf16[32,2,19456]{2,1,0:T(2,128)(2,1)} fusion(bf16[32,2,19456]{2,1,0:T(2,128)(2,1)} %get-tuple-element.99, s32[]{:T(128)} %get-tuple-element.96, bf16[2,32,19584]{2,0,1:T(2,128)(2,1)S(1)} %get-tuple-element.102, s32[]{:T(128)} %bitcast.73, s32[]{:T(128)} %bitcast.74), kind=kLoop, calls=%fused_computation.2.clone.1 | loop fusion | bytes 157184 | tf_op jit(solution)/shard_map/vmap(vmap())/gather
  93.6 2.0 %bitcast_dynamic-update-slice_fusion.2 = bf16[32,2,19456]{2,1,0:T(2,128)(2,1)} fusion(bf16[32,2,19456]{2,1,0:T(2,128)(2,1)} %get-tuple-element.99, s32[]{:T(128)} %get-tuple-element.96, bf16[2,32,19584]{2,0,1:T(2,128)(2,1)S(1)} %get-tuple-element.102, s32[]{:T(128)} %bitcast.73, s32[]{:T(128)} %bitcast.74), kind=kLoop, calls=%fused_computation.2.clone.1 | loop fusion | bytes 157184 | tf_op jit(solution)/shard_map/vmap(vmap())/gather
  96.2 2.0 %bitcast_dynamic-update-slice_fusion.2 = bf16[32,2,19456]{2,1,0:T(2,128)(2,1)} fusion(bf16[32,2,19456]{2,1,0:T(2,128)(2,1)} %get-tuple-element.99, s32[]{:T(128)} %get-tuple-element.96, bf16[2,32,19584]{2,0,1:T(2,128)(2,1)S(1)} %get-tuple-element.102, s32[]{:T(128)} %bitcast.73, s32[]{:T(128)} %bitcast.74), kind=kLoop, calls=%fused_computation.2.clone.1 | loop fusion | bytes 157184 | tf_op jit(solution)/shard_map/vmap(vmap())/gather
  98.8 2.0 %bitcast_dynamic-update-slice_fusion.2 = bf16[32,2,19456]{2,1,0:T(2,128)(2,1)} fusion(bf16[32,2,19456]{2,1,0:T(2,128)(2,1)} %get-tuple-element.99, s32[]{:T(128)} %get-tuple-element.96, bf16[2,32,19584]{2,0,1:T(2,128)(2,1)S(1)} %get-tuple-element.102, s32[]{:T(128)} %bitcast.73, s32[]{:T(128)} %bitcast.74), kind=kLoop, calls=%fused_computation.2.clone.1 | loop fusion | bytes 157184 | tf_op jit(solution)/shard_map/vmap(vmap())/gather
  101.4 2.0 %bitcast_dynamic-update-slice_fusion.2 = bf16[32,2,19456]{2,1,0:T(2,128)(2,1)} fusion(bf16[32,2,19456]{2,1,0:T(2,128)(2,1)} %get-tuple-element.99, s32[]{:T(128)} %get-tuple-element.96, bf16[2,32,19584]{2,0,1:T(2,128)(2,1)S(1)} %get-tuple-element.102, s32[]{:T(128)} %bitcast.73, s32[]{:T(128)} %bitcast.74), kind=kLoop, calls=%fused_computation.2.clone.1 | loop fusion | bytes 157184 | tf_op jit(solution)/shard_map/vmap(vmap())/gather
  103.4 3.6 %copy.25 = bf16[2,32,19456]{2,1,0:T(8,128)(2,1)} copy(bf16[2,32,19456]{2,0,1:T(2,128)(2,1)} %bitcast.75) | data formatting | bytes 4980736 | tf_op jit(solution)/shard_map/vmap(vmap())/gather | solution.py:17
  107.0 3.3 %reshape.45 = bf16[2,32,19,1024]{3,2,1,0:T(8,128)(2,1)S(1)} reshape(bf16[2,32,19456]{2,1,0:T(8,128)(2,1)} %copy.25) | data formatting | bytes 4980736 | tf_op jit(solution)/shard_map/reshape | solution.py:20
  110.4 5.1 %add_convert_fusion = bf16[2,32,4,1024]{3,2,1,0:T(4,128)(2,1)} fusion(bf16[2,32,19,1024]{3,2,1,0:T(8,128)(2,1)S(1)} %reshape.45, f32[1024]{0:T(1024)S(1)} %bitcast.96, f32[1024]{0:T(1024)S(1)} %bitcast.95, f32[1024]{0:T(1024)S(1)} %bitcast.94, f32[1024]{0:T(1024)S(1)} %bitcast.93, f32[1024]{0:T(1024)S(1)} %bitcast.92, f32[1024]{0:T(1024)S(1)} %bitcast.91, ...), kind=kLoop, calls=%fused_computation.26 | loop fusion | flops 12582912 | bytes 8978432 | tf_op jit(solution)/shard_map/convert_element_type | solution.py:27
  115.5 1.2 reshape.46
  116.6 4.8 %fusion.1 = f32[256,2048]{1,0:T(8,128)S(1)} fusion(bf16[256,1024]{1,0:T(8,128)(2,1)S(1)} %reshape.46, f32[1024,1024]{1,0:T(8,128)} %get-tuple-element.57, f32[1024,1024]{1,0:T(8,128)} %get-tuple-element.58), kind=kOutput, calls=%fused_computation.10 | convolution fusion | flops 1082130432 | bytes 11010048 | tf_op jit(solution)/shard_map/dot_general | solution.py:40
  121.5 1.0 copy-done.1
  122.5 1.3 fusion.10
  123.9 2.8 %reshape.47 = f32[2,32,4,2,1024]{4,3,2,1,0:T(2,128)} reshape(f32[256,2048]{1,0:T(8,128)S(1)} %fusion.10) | data formatting | bytes 4194304 | tf_op jit(solution)/shard_map/reshape | solution.py:42
  126.7 5.4 %fusion.17 = (f32[1,32,4,1,1024]{4,3,2,1,0:T(1,128)S(1)}, f32[1,32,4,1,1024]{4,3,2,1,0:T(1,128)S(1)}, f32[1,32,4,1,1024]{4,3,2,1,0:T(1,128)}, f32[1,32,4,1,1024]{4,3,2,1,0:T(1,128)}) fusion(f32[2,32,4,2,1024]{4,3,2,1,0:T(2,128)} %reshape.47), kind=kLoop, calls=%fused_computation.44 | loop fusion | bytes 4194304 | tf_op jit(solution)/shard_map/slice | solution.py:44
  132.1 2.7 %copy.38 = f32[1,32,4,1,1024]{1,2,4,3,0:T(4,128)S(1)} copy(f32[1,32,4,1,1024]{4,3,2,1,0:T(1,128)} %get-tuple-element.36) | data formatting | bytes 1048576
  134.8 3.3 %copy.39 = f32[1,32,4,1,1024]{1,2,4,3,0:T(4,128)} copy(f32[1,32,4,1,1024]{4,3,2,1,0:T(1,128)} %get-tuple-element.35) | data formatting | bytes 1048576
  138.1 2.4 %copy.40 = f32[1,32,4,1,1024]{1,2,4,3,0:T(4,128)} copy(f32[1,32,4,1,1024]{4,3,2,1,0:T(1,128)S(1)} %get-tuple-element.34) | data formatting | bytes 1048576
  140.5 2.4 %copy.41 = f32[1,32,4,1,1024]{1,2,4,3,0:T(4,128)} copy(f32[1,32,4,1,1024]{4,3,2,1,0:T(1,128)S(1)} %get-tuple-element.33) | data formatting | bytes 1048576
  142.9 5.7 %add_reduce_fusion = (f32[32,1024]{0,1:T(8,128)S(1)}, bf16[32,4,1024]{0,1,2:T(4,128)(2,1)}, bf16[32,4,1024]{0,1,2:T(4,128)(2,1)}) fusion(f32[1,32,4,1,1024]{1,2,4,3,0:T(4,128)S(1)} %copy.38, f32[1,32,4,1,1024]{1,2,4,3,0:T(4,128)} %copy.39, f32[1,32,4,1,1024]{1,2,4,3,0:T(4,128)} %copy.40, f32[1,32,4,1,1024]{1,2,4,3,0:T(4,128)} %copy.41), kind=kLoop, calls=%fused_computation.21 | loop fusion | flops 1015808 | bytes 2752512 | tf_op jit(solution)/shard_map/reduce_sum | solution.py:63
  148.6 1.8 gather_fusion.1
  150.4 1.8 gather_fusion
  152.2 0.7 reshape.88
  152.9 4.2 %all-to-all-start = ((bf16[4,2,512]{2,1,0:T(2,128)(2,1)}), bf16[4,2,512]{2,1,0:T(2,128)(2,1)S(1)}, u32[]{:S(2)}, u32[]{:S(2)}) async-start(bf16[4,2,512]{2,1,0:T(2,128)(2,1)} %reshape.88), calls=%async_computation | async-start | bytes 16384 | tf_op jit(solution)/shard_map/all_to_all | solution.py:70
  157.2 1.6 fusion.18
  158.8 0.8 copy.37
  159.5 1.5 all-to-all-done
  161.2 31.3 %all_gather.7 = bf16[8,2,4,4,128]{4,3,2,1,0:T(4,128)(2,1)S(1)} all-gather(bf16[1,2,4,4,128]{4,3,2,1,0:T(4,128)(2,1)S(1)} %all_gather.6), channel_id=1, replica_groups=mesh['elem'=8,'chan'=4] {'elem'}, dimensions={0}, use_global_device_ids=true | all-gather | bytes 73728 | tf_op jit(solution)/shard_map/all_gather | solution.py:72
  193.8 0.6 pad_maximum_fusion.1
  (91 shorter events, 17.5 us)
Async XLA Ops:
  0.6 17.8 %copy-start.3 = (bf16[16,1024]{1,0:T(8,128)(2,1)S(1)}, bf16[16,1024]{1,0:T(8,128)(2,1)}, u32[]{:S(2)}) copy-start(bf16[16,1024]{1,0:T(8,128)(2,1)} %param.7) | copy-start | bytes 98308
  0.7 17.9 %copy-start.2 = (bf16[2,32,19584]{2,1,0:T(8,128)(2,1)S(1)}, bf16[2,32,19584]{2,1,0:T(8,128)(2,1)}, u32[]{:S(2)}) copy-start(bf16[2,32,19584]{2,1,0:T(8,128)(2,1)} %param.5) | copy-start | bytes 7520260
  18.5 2.0 %copy-start.4 = (s32[32]{0:T(128)S(1)}, s32[32]{0:T(128)}, u32[]{:S(2)}) copy-start(s32[32]{0:T(128)} %param.6) | copy-start | bytes 388
  116.6 4.9 %copy-start = (f32[1024,1024]{1,0:T(8,128)S(1)}, f32[1024,1024]{1,0:T(8,128)}, u32[]{:S(2)}) copy-start(f32[1024,1024]{1,0:T(8,128)} %get-tuple-element.57) | copy-start | bytes 12582916
  116.6 5.9 %copy-start.1 = (f32[1024,1024]{1,0:T(8,128)S(1)}, f32[1024,1024]{1,0:T(8,128)}, u32[]{:S(2)}) copy-start(f32[1024,1024]{1,0:T(8,128)} %get-tuple-element.58) | copy-start | bytes 12582916
  134.8 8.1 %copy-start.5 = (s32[16]{0:T(128)S(1)}, s32[16]{0:T(128)}, u32[]{:S(2)}) copy-start(s32[16]{0:T(128)} %param.8) | copy-start | bytes 196
  152.9 8.1 %all-to-all-start = ((bf16[4,2,512]{2,1,0:T(2,128)(2,1)}), bf16[4,2,512]{2,1,0:T(2,128)(2,1)S(1)}, u32[]{:S(2)}, u32[]{:S(2)}) async-start(bf16[4,2,512]{2,1,0:T(2,128)(2,1)} %reshape.88), calls=%async_computation | async-start | bytes 16384 | tf_op jit(solution)/shard_map/all_to_all | solution.py:70
